TPU v7x, 32 devices: a whole 2x2x4 slice. The times are simulated.
32 devices in a mesh: dp: 4 (over y, core), tensor: 8 (over z, x).
Axes of the slice: x: 2, y: 2, z: 4, core: 2. Of those that a mesh axis runs over, the one named last changes fastest.
Arguments:
- grads: bfloat16 [4, 2, 7168, 2048], P('dp', None, 'tensor'), may hold values from -6 to 6
- master: float32 [2, 7168, 2048], P(None, 'dp', 'tensor'), may hold values from -0.0625 to 0.0625
- moment1: float32 [2, 7168, 2048], P(None, 'dp', 'tensor'), may hold values from -3 to 3
- moment2: float32 [2, 7168, 2048], P(None, 'dp', 'tensor'), may hold values from 1 to 30
- tokens: bfloat16 [1024, 7168], P('dp'), may hold values from -6 to 6
- route: int32 [512], P('dp'), may hold values from 0 to 255, as said below
Outputs:
- new_master: float32 [2, 7168, 2048], P(None, 'dp', 'tensor')
- new_moment1: float32 [2, 7168, 2048], P(None, 'dp', 'tensor')
- new_moment2: float32 [2, 7168, 2048], P(None, 'dp', 'tensor')
- rollout: bfloat16 [2, 7168, 2048], P(None, None, 'tensor')
- hidden: bfloat16 [512, 2048], P('dp', 'tensor')
Inputs may be any that keep to these rules, and one draw needn't show every extreme that they name: route[i] indexes one of the 256 tokens of the data rank that holds routed row i; within one data rank's 128 routed rows no token appears twice.
All inputs are finite; a program needn't handle non-finite values.
Results may differ from a plain program's by a relative error of at most 0.019.
Values may be sent and summed in bfloat16 or wider, within the bound.
A program may use at most 128 MiB of HBM per device.

v0:
```python
import functools

import jax
import jax.numpy as jnp
from jax import lax
from jax.experimental import pallas as pl
from jax.experimental.pallas import tpu as pltpu
from jax.sharding import PartitionSpec as P

MESH = pl.DeviceIdType.MESH
LANES = 128
CHUNK = 64
AHEAD = 4


def body(grads, master, moment1, moment2, tokens, route):
    tensor_count = lax.axis_size("tensor")
    rank_count = lax.axis_size("dp")
    grad_local = grads[0]
    rows_tensor = grad_local.shape[1]
    hidden_width = grad_local.shape[2]
    col_width = hidden_width // tensor_count
    slab = rows_tensor // rank_count
    summed = lax.psum_scatter(grad_local, "dp", scatter_dimension=1, tiled=True).astype(jnp.float32)
    pieces = summed.reshape(2, slab, tensor_count, col_width)
    spread = lax.all_to_all(
        pieces.astype(jnp.bfloat16), "tensor", split_axis=2, concat_axis=1, tiled=True
    ).astype(pieces.dtype)
    spread = spread.reshape(2, rank_count, tensor_count // rank_count, slab, col_width)
    owned = lax.all_to_all(
        spread.astype(jnp.bfloat16), "dp", split_axis=1, concat_axis=3, tiled=True
    ).astype(spread.dtype)
    grad_total = owned.reshape(2, rows_tensor * tensor_count // rank_count, col_width)
    new_moment1 = 0.9 * moment1 + 0.1 * grad_total
    new_moment2 = 0.95 * moment2 + 0.05 * grad_total * grad_total
    first_fix = 1.0 - 0.9**10
    second_fix = 1.0 - 0.95**10
    step_size = (
        new_moment1 / first_fix / (jnp.sqrt(new_moment2 / second_fix) + 1e-08) + 0.1 * master
    )
    new_master = master - 0.003 * step_size
    rollout_shard = new_master.astype(jnp.bfloat16)
    replicated = lax.all_gather(rollout_shard, "dp", axis=1, tiled=True)
    picked = jnp.take(tokens, route, axis=0)
    both = jnp.einsum("rd,kdh->rkh", picked, replicated, preferred_element_type=jnp.float32)
    hidden = (jax.nn.silu(both[:, 0, :]) * both[:, 1, :]).astype(jnp.bfloat16)
    return (new_master, new_moment1, new_moment2, replicated, hidden)


def kernel(
    tensor_count,
    grads,
    states,
    tokens,
    route,
    held,
    roll,
    hidden,
    mine,
    theirs,
    land,
    crossed,
    token_rows,
    picked,
    chosen,
    acc,
    load_sem,
    core_send,
    core_recv,
    state_sem,
    token_sem,
    spread_send,
    spread_recv,
    cross_send,
    cross_recv,
    near_send,
    near_recv,
    far_send,
    far_recv,
    relay_send,
    relay_recv,
):
    rank = lax.axis_index("dp")
    place = lax.axis_index("tensor")
    row, core = rank // 2, rank % 2
    near = row * 2 + 1 - core
    far = (1 - row) * 2 + core
    across = (1 - row) * 2 + 1 - core
    subs = land.shape[1]
    slab = mine.shape[0]
    width = land.shape[4]
    chunk = CHUNK
    steps = slab // chunk
    pairs = slab // LANES
    owner, sub = place // subs, place % subs
    owner_row, owner_core = owner // 2, owner % 2
    side = (owner_row + row) % 2

    def rows(step):
        return pl.ds(pl.multiple_of(step * chunk, chunk), chunk)

    def remote(source, target, send, recv, to_rank, to_place):
        return pltpu.make_async_remote_copy(
            src_ref=source,
            dst_ref=target,
            send_sem=send,
            recv_sem=recv,
            device_id=(to_rank, to_place),
            device_id_type=MESH,
        )

    def load(step):
        return pltpu.make_async_copy(
            grads.at[0, core, rows(step)], mine.at[rows(step)], load_sem.at[step]
        )

    def swap(step):
        return remote(
            grads.at[0, 1 - core, rows(step)],
            theirs.at[rows(step)],
            core_send.at[step],
            core_recv.at[step],
            near,
            place,
        )

    def state(which, step):
        return pltpu.make_async_copy(
            states[which].at[:, :, rows(step)],
            held[which].at[:, :, rows(step)],
            state_sem.at[which * steps + step],
        )

    def landing(step, part, piece, half):
        return ((step * 2 + part) * subs + piece) * 2 + half

    def spread(step, offset):
        goal = (place + offset) % tensor_count
        return remote(
            mine.at[rows(step), pl.ds(pl.multiple_of(goal * width, width), width)],
            land.at[side, sub, core, rows(step)],
            spread_send.at[step * tensor_count + offset],
            spread_recv.at[landing(step, side, sub, core)],
            row * 2 + owner_core,
            goal,
        )

    def spread_self(step):
        return pltpu.make_async_copy(
            mine.at[rows(step), pl.ds(pl.multiple_of(place * width, width), width)],
            land.at[side, sub, core, rows(step)],
            spread_recv.at[landing(step, side, sub, core)],
        )

    def wait_landing(step, part):
        for piece in range(subs):
            for half in range(2):
                spot = land.at[part, piece, half, rows(step)]
                pltpu.make_async_copy(
                    spot, spot, spread_recv.at[landing(step, part, piece, half)]
                ).wait()

    def cross(step):
        return remote(
            land.at[1, :, :, rows(step)],
            crossed.at[:, :, rows(step)],
            cross_send.at[step],
            cross_recv.at[step],
            far,
            place,
        )

    def block(of_rank, step):
        return roll.at[:, pl.ds(of_rank * subs, subs), rows(step)]

    def to_near(of_rank, step):
        return remote(
            block(of_rank, step), block(of_rank, step),
            near_send.at[step], near_recv.at[step], near, place,
        )

    def to_far(of_rank, step):
        return remote(
            block(of_rank, step), block(of_rank, step),
            far_send.at[step], far_recv.at[step], far, place,
        )

    def relay(of_rank, step):
        return remote(
            block(of_rank, step), block(of_rank, step),
            relay_send.at[step], relay_recv.at[step], near, place,
        )

    middle = tensor_count // 2
    order = sorted(range(1, tensor_count), key=lambda i: -abs(i - middle))

    def issue(step):
        load(step).wait()
        swap(step).wait_recv()
        strip = 16

        @pl.loop(0, chunk // strip)
        def _(i):
            at = pl.ds(pl.multiple_of(step * chunk + i * strip, strip), strip)
            total = mine[at].astype(jnp.float32) + theirs[at].astype(jnp.float32)
            mine[at] = total.astype(mine.dtype)

        for offset in order:
            spread(step, offset).start()

        @pl.when(owner_core == core)
        def _():
            spread_self(step).start()

        @pl.when(owner_core != core)
        def _():
            spread(step, 0).start()

    def issued(step):
        for offset in order:
            spread(step, offset).wait_send()

        @pl.when(owner_core != core)
        def _():
            spread(step, 0).wait_send()

    first_fix = 1.0 - 0.9**10
    second_fix = 1.0 - 0.95**10

    def update(step):
        wait_landing(step, 0)
        cross(step).wait_recv()
        for which in range(3):
            state(which, step).wait()
        strip = 16
        tiles = chunk // strip

        @pl.loop(0, tiles)
        def _(i):
            at = pl.ds(pl.multiple_of(step * chunk + i * strip, strip), strip)
            for half in range(2):
                for piece in range(subs):
                    grad = land[0, piece, half, at].astype(jnp.float32)
                    grad = grad + crossed[piece, half, at].astype(jnp.float32)
                    old = held[0][half, piece, at]
                    moment1 = 0.9 * held[1][half, piece, at] + 0.1 * grad
                    moment2 = 0.95 * held[2][half, piece, at] + 0.05 * grad * grad
                    scaled = jnp.sqrt(moment2 * (1.0 / second_fix)) + 1e-08
                    change = moment1 * (1.0 / first_fix) / scaled + 0.1 * old
                    new = old - 0.003 * change
                    held[0][half, piece, at] = new
                    held[1][half, piece, at] = moment1
                    held[2][half, piece, at] = moment2
                    roll[half, rank * subs + piece, at] = new.astype(roll.dtype)

        to_far(rank, step).start()
        to_near(rank, step).start()

    def pass_on(step):
        to_far(far, step).wait_recv()
        relay(far, step).start()

    def multiply(pair):
        for part in range(LANES // chunk):
            step = pair * (LANES // chunk) + part
            to_near(near, step).wait_recv()
            relay(across, step).wait_recv()
        at = pl.ds(pl.multiple_of(pair * LANES, LANES), LANES)
        for half in range(2):
            weights = roll[half, :, at].reshape(tensor_count * LANES, width)
            acc[half] += jnp.dot(
                picked[pair], weights, preferred_element_type=jnp.float32
            )

    def pick(pair):
        for part in range(tensor_count):
            at = pl.ds(pl.multiple_of(part * slab + pair * LANES, LANES), LANES)
            some = jnp.dot(
                chosen[...], token_rows[:, at], preferred_element_type=jnp.float32
            )
            picked[pair, :, part * LANES : (part + 1) * LANES] = some.astype(picked.dtype)

    @pl.loop(0, steps)
    def _(step):
        swap(step).start()
        load(step).start()

    token_copy = pltpu.make_async_copy(tokens, token_rows, token_sem)
    for ahead in range(AHEAD):
        issue(ahead)
    token_copy.start()

    @pl.loop(0, steps)
    def _(step):
        for which in range(3):
            state(which, step).start()

    acc[...] = jnp.zeros_like(acc)
    index = lax.broadcasted_iota(jnp.int32, (token_rows.shape[0], route.shape[1]), 0)
    onehot = jnp.where(index == route[...], 1.0, 0.0)
    chosen[...] = onehot.T.astype(chosen.dtype)
    per = LANES // chunk

    @pl.loop(0, steps + 4)
    def _(now):
        @pl.when(now < steps)
        def _():
            wait_landing(now, 1)
            cross(now).start()
            issued(now)

        @pl.when(now < steps - AHEAD)
        def _():
            issue(now + AHEAD)

        @pl.when(now == 0)
        def _():
            token_copy.wait()

        @pl.when(now < pairs)
        def _():
            pick(now)

        @pl.when((now >= 1) & (now < steps + 1))
        def _():
            update(now - 1)

        @pl.when((now >= 3) & (now < steps + 3))
        def _():
            pass_on(now - 3)

        @pl.when((now >= 4) & ((now - 4) % per == per - 1))
        def _():
            multiply((now - 4) // per)

    gate, up = acc[0], acc[1]
    hidden[...] = (gate / (1.0 + jnp.exp(-gate)) * up).astype(hidden.dtype)

    @pl.loop(0, steps)
    def _(step):
        swap(step).wait_send()
        cross(step).wait_send()
        to_far(rank, step).wait_send()
        to_near(rank, step).wait_send()
        relay(far, step).wait_send()


def entry(tensor_count, grads, s0, s1, s2, tokens, route, o0, o1, o2, *rest):
    kernel(tensor_count, grads, (s0, s1, s2), tokens, route, (o0, o1, o2), *rest)


def fused(grads, master, moment1, moment2, tokens, route):
    tensor_count = lax.axis_size("tensor")
    rank_count = lax.axis_size("dp")
    subs = tensor_count // rank_count
    slab, hidden_width = grads.shape[2:]
    width = hidden_width // tensor_count
    steps = slab // CHUNK
    routed = route.shape[0]
    split = (2, subs, slab, width)
    states = [array.reshape(split) for array in (master, moment1, moment2)]
    anywhere = pl.BlockSpec(memory_space=pl.ANY)
    vmem = pl.BlockSpec(memory_space=pltpu.VMEM)
    dma = pltpu.SemaphoreType.DMA
    half = jnp.bfloat16
    f32 = jnp.float32
    new_master, new1, new2, rollout, hidden = pl.pallas_call(
        functools.partial(entry, tensor_count),
        out_shape=[pltpu.VMEM(split, f32)] * 3
        + [
            pltpu.VMEM((2, tensor_count, slab, width), half),
            pltpu.VMEM((routed, width), half),
        ],
        in_specs=[anywhere] * 5 + [vmem],
        out_specs=[vmem] * 5,
        scratch_shapes=[
            pltpu.VMEM((slab, hidden_width), half),
            pltpu.VMEM((slab, hidden_width), half),
            pltpu.VMEM((2, subs, 2, slab, width), half),
            pltpu.VMEM((subs, 2, slab, width), half),
            pltpu.VMEM(tokens.shape, half),
            pltpu.VMEM((slab // LANES, routed, tensor_count * LANES), half),
            pltpu.VMEM((routed, tokens.shape[0]), half),
            pltpu.VMEM((2, routed, width), f32),
            dma((steps,)),
            dma((steps,)),
            dma((steps,)),
            dma((3 * steps,)),
            dma,
            dma((steps * tensor_count,)),
            dma((steps * 2 * subs * 2,)),
        ]
        + [dma((steps,))] * 8,
        compiler_params=pltpu.CompilerParams(
            has_side_effects=True, vmem_limit_bytes=45 * 1024 * 1024
        ),
    )(grads, *states, tokens, route.reshape(1, routed))
    whole = (2, subs * slab, width)
    return (
        new_master.reshape(whole),
        new1.reshape(whole),
        new2.reshape(whole),
        rollout.reshape(2, tensor_count * slab, width),
        hidden,
    )


def chosen_body(grads, *rest):
    tensor_count, rank_count = lax.axis_size("tensor"), lax.axis_size("dp")
    slab, hidden_width = grads.shape[2:]
    fits = (
        rank_count == 4
        and tensor_count % rank_count == 0
        and slab % LANES == 0
        and slab // CHUNK > AHEAD
        and hidden_width % (tensor_count * LANES) == 0
    )
    return fused(grads, *rest) if fits else body(grads, *rest)


def solution(mesh):
    in_specs = (
        P("dp", None, "tensor", None),
        P(None, "dp", "tensor"),
        P(None, "dp", "tensor"),
        P(None, "dp", "tensor"),
        P("dp", None),
        P("dp"),
    )
    out_specs = (
        P(None, "dp", "tensor"),
        P(None, "dp", "tensor"),
        P(None, "dp", "tensor"),
        P(None, None, "tensor"),
        P("dp", "tensor"),
    )
    return jax.shard_map(chosen_body, mesh=mesh, in_specs=in_specs, out_specs=out_specs, check_vma=False)
```

profile of v0, /device:TPU:0, one launch (start us, length us, event | category | flops | bytes accessed | tf_op | source)
XLA Modules:
  0.0 126.3 jit_solution(8802853111442607987)
XLA Ops:
  0.6 116.4 %shard_map.101 = (f32[2,2,896,256]{3,2,1,0:T(8,128)S(1)}, f32[2,2,896,256]{3,2,1,0:T(8,128)S(1)}, f32[2,2,896,256]{3,2,1,0:T(8,128)S(1)}, bf16[2,8,896,256]{3,2,1,0:T(8,128)(2,1)S(1)}, bf16[128,256]{1,0:T(8,128)(2,1)S(1)}) custom-call(bf16[1,2,896,2048]{3,2,1,0:T(8,128)(2,1)} %grads.1, f32[2,2,896,256]{3,2,1,0:T(8,128)} %bitcast.12, ...), custom_call_target="tpu_custom_call" | custom-call | tf_op jit(solution)/shard_map/pallas_call | solution.py:367
  117.1 1.8 %copy.16 = f32[2,1792,256]{2,1,0:T(8,128)} copy(f32[2,1792,256]{2,1,0:T(8,128)S(1)} %bitcast.11) | data formatting | bytes 7340032
  118.9 1.8 %copy.17 = f32[2,1792,256]{2,1,0:T(8,128)} copy(f32[2,1792,256]{2,1,0:T(8,128)S(1)} %bitcast.10) | data formatting | bytes 7340032
  120.8 0.6 copy.20
  121.4 1.8 %copy.18 = f32[2,1792,256]{2,1,0:T(8,128)} copy(f32[2,1792,256]{2,1,0:T(8,128)S(1)} %bitcast.9) | data formatting | bytes 7340032
  123.2 3.0 %copy.19 = bf16[2,7168,256]{2,1,0:T(8,128)(2,1)} copy(bf16[2,7168,256]{2,1,0:T(8,128)(2,1)S(1)} %bitcast.8) | data formatting | bytes 14680064
where the time goes:
time: 127 us; the launch traced here: 126 us
  Pallas kernels  116 us (91%)
  local copies, waits for them, and re-layouts  9.19 us (7%)
    pallas_call x1, Pallas kernels, fused(): pl.pallas_call(functools.partial(entry, tensor_count), out_shape=[pltpu.V...  116 us
    unnamed x5, local copies, waits for them, and re-layouts  9.19 us

commit v1 on v0

v1 whole, which is shorter than its diff:
```python
import functools

import jax
import jax.numpy as jnp
from jax import lax
from jax.experimental import pallas as pl
from jax.experimental.pallas import tpu as pltpu
from jax.sharding import PartitionSpec as P

MESH = pl.DeviceIdType.MESH
LANES = 128
CHUNK = 32
AHEAD = 4
LEAD = 3
LATE = 3
STRIP = 16


def body(grads, master, moment1, moment2, tokens, route):
    tensor_count = lax.axis_size("tensor")
    rank_count = lax.axis_size("dp")
    grad_local = grads[0]
    rows_tensor = grad_local.shape[1]
    hidden_width = grad_local.shape[2]
    col_width = hidden_width // tensor_count
    slab = rows_tensor // rank_count
    summed = lax.psum_scatter(grad_local, "dp", scatter_dimension=1, tiled=True).astype(jnp.float32)
    pieces = summed.reshape(2, slab, tensor_count, col_width)
    spread = lax.all_to_all(
        pieces.astype(jnp.bfloat16), "tensor", split_axis=2, concat_axis=1, tiled=True
    ).astype(pieces.dtype)
    spread = spread.reshape(2, rank_count, tensor_count // rank_count, slab, col_width)
    owned = lax.all_to_all(
        spread.astype(jnp.bfloat16), "dp", split_axis=1, concat_axis=3, tiled=True
    ).astype(spread.dtype)
    grad_total = owned.reshape(2, rows_tensor * tensor_count // rank_count, col_width)
    new_moment1 = 0.9 * moment1 + 0.1 * grad_total
    new_moment2 = 0.95 * moment2 + 0.05 * grad_total * grad_total
    first_fix = 1.0 - 0.9**10
    second_fix = 1.0 - 0.95**10
    step_size = (
        new_moment1 / first_fix / (jnp.sqrt(new_moment2 / second_fix) + 1e-08) + 0.1 * master
    )
    new_master = master - 0.003 * step_size
    rollout_shard = new_master.astype(jnp.bfloat16)
    replicated = lax.all_gather(rollout_shard, "dp", axis=1, tiled=True)
    picked = jnp.take(tokens, route, axis=0)
    both = jnp.einsum("rd,kdh->rkh", picked, replicated, preferred_element_type=jnp.float32)
    hidden = (jax.nn.silu(both[:, 0, :]) * both[:, 1, :]).astype(jnp.bfloat16)
    return (new_master, new_moment1, new_moment2, replicated, hidden)


def reduce_kernel(
    tensor_count,
    grads,
    state0,
    state1,
    state2,
    tokens,
    route,
    held0,
    held1,
    held2,
    roll,
    picked,
    mine,
    theirs,
    land,
    inward,
    token_rows,
    chosen,
    load_sem,
    swap_send,
    swap_recv,
    state_sem,
    token_sem,
    apart_send,
    same_send,
    land_recv,
    inward_send,
    inward_recv,
    cross_send,
    cross_recv,
    near_send,
    near_recv,
    far_send,
    far_recv,
    relay_send,
    relay_recv,
):
    states, held = (state0, state1, state2), (held0, held1, held2)
    rank = lax.axis_index("dp")
    place = lax.axis_index("tensor")
    row, core = rank // 2, rank % 2
    near = row * 2 + 1 - core
    far = (1 - row) * 2 + core
    subs = land.shape[1]
    slab = mine.shape[0]
    width = land.shape[4]
    chunk = CHUNK
    steps = slab // chunk
    owner, sub = place // subs, place % subs
    side, owner_core = owner // 2, owner % 2
    group = 2 * subs
    span = group * width
    home = row == side
    away = row != side
    same_cols = pl.ds(pl.multiple_of(side * span, span), span)
    apart_cols = pl.ds(pl.multiple_of((1 - side) * span, span), span)
    slot = jnp.where(home, 0, 1)

    def rows(step):
        return pl.ds(pl.multiple_of(step * chunk, chunk), chunk)

    def columns(goal):
        return pl.ds(pl.multiple_of(goal * width, width), width)

    def remote(source, target, send, recv, to_rank, to_place):
        return pltpu.make_async_remote_copy(
            src_ref=source,
            dst_ref=target,
            send_sem=send,
            recv_sem=recv,
            device_id=(to_rank, to_place),
            device_id_type=MESH,
        )

    def arrived(spot, sem):
        pltpu.make_async_copy(spot, spot, sem).wait()

    def load(step):
        return pltpu.make_async_copy(
            grads.at[0, core, rows(step)], mine.at[rows(step)], load_sem.at[step]
        )

    def swap(step):
        return remote(
            grads.at[0, 1 - core, rows(step)], theirs.at[rows(step)],
            swap_send.at[step], swap_recv.at[step], near, place,
        )

    def state(which, step):
        return pltpu.make_async_copy(
            states[which].at[:, :, rows(step)],
            held[which].at[:, :, rows(step)],
            state_sem.at[which * steps + step],
        )

    def inbound(step):
        return remote(
            mine.at[rows(step), same_cols], inward.at[rows(step)],
            inward_send.at[step], inward_recv.at[step], far, place,
        )

    def spread_apart(step, offset):
        goal = (1 - side) * group + (place + offset) % group
        return remote(
            mine.at[rows(step), columns(goal)],
            land.at[slot, sub, core, rows(step)],
            apart_send.at[step],
            land_recv.at[slot * steps + step],
            row * 2 + owner_core,
            goal,
        )

    def spread_same(step, offset):
        goal = side * group + (place + offset) % group
        return remote(
            mine.at[rows(step), columns(goal)],
            land.at[0, sub, core, rows(step)],
            same_send.at[step],
            land_recv.at[step],
            row * 2 + owner_core,
            goal,
        )

    def spread_self(step):
        return pltpu.make_async_copy(
            mine.at[rows(step), columns(place)],
            land.at[0, sub, core, rows(step)],
            land_recv.at[step],
        )

    def landed(step, part):
        arrived(land.at[part, :, :, rows(step)], land_recv.at[part * steps + step])

    def cross(step):
        return remote(
            land.at[1, :, :, rows(step)], land.at[1, :, :, rows(step)],
            cross_send.at[step], cross_recv.at[step], far, place,
        )

    def block(of_rank, step):
        return roll.at[:, pl.ds(of_rank * subs, subs), rows(step)]

    def to_near(of_rank, step):
        return remote(
            block(of_rank, step), block(of_rank, step),
            near_send.at[step], near_recv.at[step], near, place,
        )

    def to_far(of_rank, step):
        return remote(
            block(of_rank, step), block(of_rank, step),
            far_send.at[step], far_recv.at[step], far, place,
        )

    def relay(of_rank, step):
        return remote(
            block(of_rank, step), block(of_rank, step),
            relay_send.at[step], relay_recv.at[step], near, place,
        )

    def fetch(step):
        load(step).wait()
        swap(step).wait_recv()

    def combine(step, cols, third=None):
        @pl.loop(0, chunk // STRIP)
        def _(i):
            at = pl.ds(pl.multiple_of(step * chunk + i * STRIP, STRIP), STRIP)
            total = mine[at, cols].astype(jnp.float32) + theirs[at, cols].astype(jnp.float32)
            if third is not None:
                total = total + third[at].astype(jnp.float32)
            mine[at, cols] = total.astype(mine.dtype)

    def issue_inward(step):
        fetch(step)
        combine(step, same_cols)
        inbound(step).start()

    def issue_apart(step):
        combine(step, apart_cols)
        for offset in range(group):
            spread_apart(step, offset).start()

    def issue_same(step):
        inbound(step).wait_recv()
        combine(step, same_cols, inward)
        for offset in range(1, group):
            spread_same(step, offset).start()

        @pl.when(owner_core == core)
        def _():
            spread_self(step).start()

        @pl.when(owner_core != core)
        def _():
            spread_same(step, 0).start()

    first_fix = 1.0 - 0.9**10
    second_fix = 1.0 - 0.95**10

    def update(step, crossed):
        for which in range(3):
            state(which, step).wait()

        @pl.loop(0, chunk // STRIP)
        def _(i):
            at = pl.ds(pl.multiple_of(step * chunk + i * STRIP, STRIP), STRIP)
            for half in range(2):
                for piece in range(subs):
                    grad = land[0, piece, half, at].astype(jnp.float32)
                    if crossed:
                        grad = grad + land[1, piece, half, at].astype(jnp.float32)
                    old = held[0][half, piece, at]
                    moment1 = 0.9 * held[1][half, piece, at] + 0.1 * grad
                    moment2 = 0.95 * held[2][half, piece, at] + 0.05 * grad * grad
                    scaled = jnp.sqrt(moment2 * (1.0 / second_fix)) + 1e-08
                    change = moment1 * (1.0 / first_fix) / scaled + 0.1 * old
                    new = old - 0.003 * change
                    held[0][half, piece, at] = new
                    held[1][half, piece, at] = moment1
                    held[2][half, piece, at] = moment2
                    roll[half, rank * subs + piece, at] = new.astype(roll.dtype)

        to_far(rank, step).start()
        to_near(rank, step).start()

    barrier = pltpu.get_barrier_semaphore()
    peers = 0
    for hop in range(tensor_count):
        goal = (place + hop) % tensor_count
        for which in range(2):
            if hop or which:
                pl.semaphore_signal(
                    barrier, inc=1, device_id=(row * 2 + (core + which) % 2, goal), device_id_type=MESH
                )
                peers += 1
    pl.semaphore_signal(barrier, inc=1, device_id=(far, place), device_id_type=MESH)
    peers += 1

    token_copy = pltpu.make_async_copy(tokens, token_rows, token_sem)
    token_copy.start()

    @pl.loop(0, steps)
    def _(step):
        load(step).start()

    index = lax.broadcasted_iota(jnp.int32, (token_rows.shape[0], route.shape[1]), 0)
    onehot = jnp.where(index == route[...], 1.0, 0.0)
    chosen[...] = onehot.T.astype(chosen.dtype)
    token_copy.wait()
    wide = tensor_count * LANES

    @pl.loop(0, token_rows.shape[1] // wide)
    def _(part):
        at = pl.ds(pl.multiple_of(part * wide, wide), wide)
        some = jnp.dot(chosen[...], token_rows[:, at], preferred_element_type=jnp.float32)
        picked[:, at] = some.astype(picked.dtype)

    pl.semaphore_wait(barrier, peers)

    @pl.loop(0, steps)
    def _(step):
        swap(step).start()

    @pl.loop(0, steps)
    def _(step):
        for which in range(3):
            state(which, step).start()

    @pl.loop(0, AHEAD)
    def _(step):
        @pl.when(away)
        def _():
            issue_inward(step)

        @pl.when(home)
        def _():
            fetch(step)

        issue_apart(step)

    @pl.when(away)
    def _():
        @pl.loop(AHEAD, AHEAD + LEAD)
        def _(step):
            issue_inward(step)

    @pl.when(home)
    def _():
        @pl.loop(0, AHEAD)
        def _(step):
            issue_same(step)

    @pl.loop(0, steps + LATE)
    def _(now):
        @pl.when(home & (now < steps))
        def _():
            landed(now, 1)
            cross(now).start()

        @pl.when(home & (now < steps - AHEAD))
        def _():
            fetch(now + AHEAD)
            issue_apart(now + AHEAD)
            issue_same(now + AHEAD)

        @pl.when(away & (now < steps - AHEAD))
        def _():
            issue_apart(now + AHEAD)

        @pl.when(away & (now < steps - AHEAD - LEAD))
        def _():
            issue_inward(now + AHEAD + LEAD)

        @pl.when(home & (now < steps))
        def _():
            landed(now, 0)
            update(now, False)

        @pl.when(away & (now < steps))
        def _():
            landed(now, 0)
            cross(now).wait_recv()
            update(now, True)

        @pl.when(now >= LATE)
        def _():
            to_far(far, now - LATE).wait_recv()
            relay(far, now - LATE).start()

    @pl.loop(0, steps)
    def _(step):
        swap(step).wait_send()
        sent = mine.at[rows(step), apart_cols]
        arrived(sent, apart_send.at[step])

        @pl.when(away)
        def _():
            inbound(step).wait_send()

        @pl.when(home)
        def _():
            cross(step).wait_send()

        @pl.when(home & (owner_core == core))
        def _():
            part = mine.at[rows(step), pl.ds(0, span - width)]
            arrived(part, same_send.at[step])

        @pl.when(home & (owner_core != core))
        def _():
            part = mine.at[rows(step), pl.ds(0, span)]
            arrived(part, same_send.at[step])

        to_far(rank, step).wait_send()
        to_near(rank, step).wait_send()
        to_near(near, step).wait_recv()
        relay(far, step).wait_send()
        relay((1 - row) * 2 + 1 - core, step).wait_recv()


def finish_kernel(
    held0, held1, held2, roll, picked, out0, out1, out2, full, hidden, acc, small, sems
):
    copies = []
    for source, target in ((held0, out0), (held1, out1), (held2, out2), (roll, full)):
        for half in range(2):
            copies.append(
                pltpu.make_async_copy(source.at[half], target.at[half], sems.at[len(copies)])
            )
    for copy in copies:
        copy.start()
    acc[...] = jnp.zeros_like(acc)
    depth = picked.shape[1]
    wide = depth // 7 if depth % (7 * LANES) == 0 else LANES

    @pl.loop(0, depth // wide)
    def _(part):
        at = pl.ds(pl.multiple_of(part * wide, wide), wide)
        for half in range(2):
            acc[half] += jnp.dot(
                picked[:, at], roll[half, at], preferred_element_type=jnp.float32
            )

    gate, up = acc[0], acc[1]
    small[...] = (gate / (1.0 + jnp.exp(-gate)) * up).astype(small.dtype)
    last = pltpu.make_async_copy(small, hidden, sems.at[len(copies)])
    last.start()
    for copy in copies:
        copy.wait()
    last.wait()


def fused(grads, master, moment1, moment2, tokens, route):
    tensor_count = lax.axis_size("tensor")
    rank_count = lax.axis_size("dp")
    subs = tensor_count // rank_count
    slab, hidden_width = grads.shape[2:]
    width = hidden_width // tensor_count
    steps = slab // CHUNK
    routed = route.shape[0]
    depth = tokens.shape[1]
    split = (2, subs, slab, width)
    states = [array.reshape(split) for array in (master, moment1, moment2)]
    anywhere = pl.BlockSpec(memory_space=pl.ANY)
    vmem = pl.BlockSpec(memory_space=pltpu.VMEM)
    hbm = pl.BlockSpec(memory_space=pltpu.HBM)
    dma = pltpu.SemaphoreType.DMA
    half = jnp.bfloat16
    f32 = jnp.float32
    parts = pl.pallas_call(
        functools.partial(reduce_kernel, tensor_count),
        out_shape=[pltpu.VMEM(split, f32)] * 3
        + [
            pltpu.VMEM((2, tensor_count, slab, width), half),
            pltpu.VMEM((routed, depth), half),
        ],
        in_specs=[anywhere] * 5 + [vmem],
        out_specs=[vmem] * 5,
        scratch_shapes=[
            pltpu.VMEM((slab, hidden_width), half),
            pltpu.VMEM((slab, hidden_width), half),
            pltpu.VMEM((2, subs, 2, slab, width), half),
            pltpu.VMEM((slab, hidden_width // 2), half),
            pltpu.VMEM(tokens.shape, half),
            pltpu.VMEM((routed, tokens.shape[0]), half),
            dma((steps,)),
            dma((steps,)),
            dma((steps,)),
            dma((3 * steps,)),
            dma,
            dma((steps,)),
            dma((steps,)),
            dma((2 * steps,)),
        ]
        + [dma((steps,))] * 10,
        compiler_params=pltpu.CompilerParams(
            has_side_effects=True, collective_id=0, vmem_limit_bytes=42 * 1024 * 1024
        ),
    )(grads, *states, tokens, route.reshape(1, routed))
    whole = (2, subs * slab, width)
    wide = (2, tensor_count * slab, width)
    *held, roll, picked = parts
    held = [array.reshape(whole) for array in held]
    new_master, new1, new2, rollout, hidden = pl.pallas_call(
        finish_kernel,
        out_shape=[pltpu.HBM(whole, f32)] * 3
        + [pltpu.HBM(wide, half), pltpu.HBM((routed, width), half)],
        in_specs=[vmem] * 5,
        out_specs=[hbm] * 5,
        scratch_shapes=[
            pltpu.VMEM((2, routed, width), f32),
            pltpu.VMEM((routed, width), half),
            dma((9,)),
        ],
        compiler_params=pltpu.CompilerParams(vmem_limit_bytes=8 * 1024 * 1024),
    )(*held, roll.reshape(wide), picked)
    return (new_master, new1, new2, rollout, hidden)


def chosen_body(grads, master, moment1, moment2, tokens, route):
    tensor_count, rank_count = lax.axis_size("tensor"), lax.axis_size("dp")
    slab, hidden_width = grads.shape[2:]
    fits = (
        rank_count == 4
        and tensor_count % rank_count == 0
        and slab % LANES == 0
        and slab % CHUNK == 0
        and slab // CHUNK > AHEAD + LEAD
        and tokens.shape[1] % (tensor_count * LANES) == 0
        and hidden_width % (tensor_count * LANES) == 0
    )
    chosen = fused if fits else body
    return chosen(grads, master, moment1, moment2, tokens, route)


def solution(mesh):
    in_specs = (
        P("dp", None, "tensor", None),
        P(None, "dp", "tensor"),
        P(None, "dp", "tensor"),
        P(None, "dp", "tensor"),
        P("dp", None),
        P("dp"),
    )
    out_specs = (
        P(None, "dp", "tensor"),
        P(None, "dp", "tensor"),
        P(None, "dp", "tensor"),
        P(None, None, "tensor"),
        P("dp", "tensor"),
    )
    return jax.shard_map(chosen_body, mesh=mesh, in_specs=in_specs, out_specs=out_specs, check_vma=False)
```

time: 127 us -> 113 us (0.89)
  local copies, waits for them, and re-layouts: 9.19 us -> 0 us
  Pallas kernels: 116 us -> 113 us
    unnamed x5 -> x0, local copies, waits for them, and re-layouts: 9.19 us -> none
    pallas_call x1 -> x2, Pallas kernels: 116 us -> 113 us  [the longest x1 106 us: fused(): pl.pallas_call(functools.partial(reduce_kernel, tensor_count), out_shape=...]
where the time goes in v1:
time: 113 us
  Pallas kernels  113 us (100%)
    pallas_call x1, Pallas kernels, fused(): pl.pallas_call(functools.partial(reduce_kernel, tensor_count), out_shape=...  106 us
    pallas_call x1, Pallas kernels, fused(): pl.pallas_call(finish_kernel, out_shape=[pltpu.HBM(whole, f32)] * 3 + [pl...  6.49 us

profile of v1, /device:TPU:0, one launch (start us, length us, event | category | flops | bytes accessed | tf_op | source)
XLA Modules:
  0.0 113.3 jit_solution(12921165073141369988)
XLA Ops:
  0.6 106.1 %shard_map.101 = (f32[2,2,896,256]{3,2,1,0:T(8,128)S(1)}, f32[2,2,896,256]{3,2,1,0:T(8,128)S(1)}, f32[2,2,896,256]{3,2,1,0:T(8,128)S(1)}, bf16[2,8,896,256]{3,2,1,0:T(8,128)(2,1)S(1)}, bf16[128,7168]{1,0:T(8,128)(2,1)S(1)}) custom-call(bf16[1,2,896,2048]{3,2,1,0:T(8,128)(2,1)} %grads.1, f32[2,2,896,256]{3,2,1,0:T(8,128)} %bitcast.12, ...), custom_call_target="tpu_custom_call" | custom-call | tf_op jit(solution)/shard_map/pallas_call | solution.py:464
  106.8 6.5 %shard_map.102 = (f32[2,1792,256]{2,1,0:T(8,128)}, f32[2,1792,256]{2,1,0:T(8,128)}, f32[2,1792,256]{2,1,0:T(8,128)}, bf16[2,7168,256]{2,1,0:T(8,128)(2,1)}, bf16[128,256]{1,0:T(8,128)(2,1)}) custom-call(f32[2,1792,256]{2,1,0:T(8,128)S(1)} %bitcast.9, f32[2,1792,256]{2,1,0:T(8,128)S(1)} %bitcast.10, f32[2,1792,256]{2,1,0:T(8,128)S(1)} %bitcast.11, ...), custom_call_target="tpu_custom_call" | custom-call | tf_op jit(solution)/shard_map/pallas_call | solution.py:498

commit v2 on v1

--- a/solution.py
+++ b/solution.py
@@ -10,10 +10,15 @@
 MESH = pl.DeviceIdType.MESH
 LANES = 128
 CHUNK = 32
-AHEAD = 4
-LEAD = 3
-LATE = 3
+AHEAD = 3
+SAME = 3
+LEAD = 8
+LATE = 4
+PRE = 3
+PICK = 4
 STRIP = 16
+SWAPS = (1, 2, 4, 8, 16)
+READY = 4
 
 
 def body(grads, master, moment1, moment2, tokens, route):
@@ -65,8 +70,10 @@
     picked,
     mine,
     theirs,
+    leaving,
     land,
     inward,
+    early,
     token_rows,
     chosen,
     load_sem,
@@ -79,8 +86,9 @@
     land_recv,
     inward_send,
     inward_recv,
+    early_send,
+    early_recv,
     cross_send,
-    cross_recv,
     near_send,
     near_recv,
     far_send,
@@ -94,6 +102,7 @@
     row, core = rank // 2, rank % 2
     near = row * 2 + 1 - core
     far = (1 - row) * 2 + core
+    across = (1 - row) * 2 + 1 - core
     subs = land.shape[1]
     slab = mine.shape[0]
     width = land.shape[4]
@@ -128,28 +137,41 @@
     def arrived(spot, sem):
         pltpu.make_async_copy(spot, spot, sem).wait()
 
-    def load(step):
+    ready = READY * chunk
+    stops = (*(stop for stop in SWAPS if stop < steps), steps)
+    pieces = tuple(zip((0, *stops[:-1]), stops))
+    late = steps - PRE
+    kept = pl.ds(0, late * chunk)
+    tail = pl.ds(late * chunk, PRE * chunk)
+
+    def load(which):
+        part = pl.ds(0, ready) if which == 0 else pl.ds(ready, slab - ready)
         return pltpu.make_async_copy(
-            grads.at[0, core, rows(step)], mine.at[rows(step)], load_sem.at[step]
-        )
-
-    def swap(step):
-        return remote(
-            grads.at[0, 1 - core, rows(step)], theirs.at[rows(step)],
-            swap_send.at[step], swap_recv.at[step], near, place,
-        )
-
-    def state(which, step):
-        return pltpu.make_async_copy(
-            states[which].at[:, :, rows(step)],
-            held[which].at[:, :, rows(step)],
-            state_sem.at[which * steps + step],
-        )
+            grads.at[0, core, part], mine.at[part], load_sem.at[which]
+        )
+
+    def bring():
+        part = pl.ds(0, ready)
+        return pltpu.make_async_copy(grads.at[0, 1 - core, part], leaving, load_sem.at[2])
+
+    def swap(piece):
+        start, stop = pieces[piece]
+        part = pl.ds(start * chunk, (stop - start) * chunk)
+        source = leaving.at[part] if stop <= READY else grads.at[0, 1 - core, part]
+        return remote(source, theirs.at[part], swap_send, swap_recv.at[piece], near, place)
+
+    def state(which):
+        return pltpu.make_async_copy(states[which], held[which], state_sem.at[which])
 
     def inbound(step):
         return remote(
             mine.at[rows(step), same_cols], inward.at[rows(step)],
-            inward_send.at[step], inward_recv.at[step], far, place,
+            inward_send, inward_recv.at[step], far, place,
+        )
+
+    def forward():
+        return remote(
+            mine.at[tail, apart_cols], early, early_send, early_recv, far, place
         )
 
     def spread_apart(step, offset):
@@ -157,7 +179,7 @@
         return remote(
             mine.at[rows(step), columns(goal)],
             land.at[slot, sub, core, rows(step)],
-            apart_send.at[step],
+            apart_send,
             land_recv.at[slot * steps + step],
             row * 2 + owner_core,
             goal,
@@ -168,7 +190,7 @@
         return remote(
             mine.at[rows(step), columns(goal)],
             land.at[0, sub, core, rows(step)],
-            same_send.at[step],
+            same_send,
             land_recv.at[step],
             row * 2 + owner_core,
             goal,
@@ -187,7 +209,7 @@
     def cross(step):
         return remote(
             land.at[1, :, :, rows(step)], land.at[1, :, :, rows(step)],
-            cross_send.at[step], cross_recv.at[step], far, place,
+            cross_send, land_recv.at[steps + step], far, place,
         )
 
     def block(of_rank, step):
@@ -196,41 +218,38 @@
     def to_near(of_rank, step):
         return remote(
             block(of_rank, step), block(of_rank, step),
-            near_send.at[step], near_recv.at[step], near, place,
+            near_send, near_recv, near, place,
         )
 
     def to_far(of_rank, step):
         return remote(
             block(of_rank, step), block(of_rank, step),
-            far_send.at[step], far_recv.at[step], far, place,
+            far_send, far_recv.at[step], far, place,
         )
 
     def relay(of_rank, step):
         return remote(
             block(of_rank, step), block(of_rank, step),
-            relay_send.at[step], relay_recv.at[step], near, place,
-        )
-
-    def fetch(step):
-        load(step).wait()
-        swap(step).wait_recv()
-
-    def combine(step, cols, third=None):
+            relay_send, relay_recv, near, place,
+        )
+
+    def combine(step, cols, third=None, base=0):
         @pl.loop(0, chunk // STRIP)
         def _(i):
             at = pl.ds(pl.multiple_of(step * chunk + i * STRIP, STRIP), STRIP)
             total = mine[at, cols].astype(jnp.float32) + theirs[at, cols].astype(jnp.float32)
             if third is not None:
-                total = total + third[at].astype(jnp.float32)
+                place_of = (step - base) * chunk + i * STRIP
+                total = total + third[pl.ds(pl.multiple_of(place_of, STRIP), STRIP)].astype(
+                    jnp.float32
+                )
             mine[at, cols] = total.astype(mine.dtype)
 
     def issue_inward(step):
-        fetch(step)
         combine(step, same_cols)
         inbound(step).start()
 
     def issue_apart(step):
-        combine(step, apart_cols)
         for offset in range(group):
             spread_apart(step, offset).start()
 
@@ -248,13 +267,15 @@
         def _():
             spread_same(step, 0).start()
 
+    def pass_on(step):
+        to_far(far, step).wait_recv()
+        relay(far, step).start()
+
+    last = steps + LATE
     first_fix = 1.0 - 0.9**10
     second_fix = 1.0 - 0.95**10
 
     def update(step, crossed):
-        for which in range(3):
-            state(which, step).wait()
-
         @pl.loop(0, chunk // STRIP)
         def _(i):
             at = pl.ds(pl.multiple_of(step * chunk + i * STRIP, STRIP), STRIP)
@@ -290,126 +311,177 @@
     pl.semaphore_signal(barrier, inc=1, device_id=(far, place), device_id_type=MESH)
     peers += 1
 
+    load(0).start()
+    bring().start()
+    load(1).start()
+    for which in range(3):
+        state(which).start()
     token_copy = pltpu.make_async_copy(tokens, token_rows, token_sem)
     token_copy.start()
-
-    @pl.loop(0, steps)
-    def _(step):
-        load(step).start()
-
     index = lax.broadcasted_iota(jnp.int32, (token_rows.shape[0], route.shape[1]), 0)
     onehot = jnp.where(index == route[...], 1.0, 0.0)
     chosen[...] = onehot.T.astype(chosen.dtype)
-    token_copy.wait()
     wide = tensor_count * LANES
-
-    @pl.loop(0, token_rows.shape[1] // wide)
-    def _(part):
+    picks = token_rows.shape[1] // wide
+
+    def pick(part):
         at = pl.ds(pl.multiple_of(part * wide, wide), wide)
         some = jnp.dot(chosen[...], token_rows[:, at], preferred_element_type=jnp.float32)
         picked[:, at] = some.astype(picked.dtype)
 
+    def pick_now(now):
+        @pl.when(now == PICK)
+        def _():
+            token_copy.wait()
+
+        @pl.when((now >= PICK) & (now < PICK + picks))
+        def _():
+            pick(now - PICK)
+
+    load(0).wait()
+    bring().wait()
     pl.semaphore_wait(barrier, peers)
-
-    @pl.loop(0, steps)
-    def _(step):
-        swap(step).start()
-
-    @pl.loop(0, steps)
-    def _(step):
+    for piece in range(len(pieces)):
+        swap(piece).start()
+
+    def first(step, action):
+        for piece, (start, _) in enumerate(pieces):
+            if start == step:
+                swap(piece).wait_recv()
+        if step == READY:
+            load(1).wait()
+        action(step)
+
+    def rest(begin):
+        for piece, (start, _) in enumerate(pieces):
+            if start >= begin:
+                swap(piece).wait_recv()
+        if begin <= READY:
+            load(1).wait()
         for which in range(3):
-            state(which, step).start()
-
-    @pl.loop(0, AHEAD)
-    def _(step):
-        @pl.when(away)
-        def _():
-            issue_inward(step)
-
-        @pl.when(home)
-        def _():
-            fetch(step)
-
+            state(which).wait()
+
+    def apart_plain(step):
+        combine(step, apart_cols)
         issue_apart(step)
+
+    @pl.when(home)
+    def _():
+        for step in range(AHEAD):
+            first(step, apart_plain)
+        rest(AHEAD)
+
+        @pl.loop(0, SAME)
+        def _(step):
+            issue_same(step)
+
+        @pl.loop(0, last)
+        def _(now):
+            @pl.when(now < late)
+            def _():
+                landed(now, 1)
+                cross(now).start()
+
+            @pl.when(now < late - AHEAD)
+            def _():
+                apart_plain(now + AHEAD)
+
+            @pl.when(now == late - AHEAD)
+            def _():
+                forward().wait_recv()
+
+            @pl.when((now >= late - AHEAD) & (now < steps - AHEAD))
+            def _():
+                combine(now + AHEAD, apart_cols, early, late)
+                issue_apart(now + AHEAD)
+
+            @pl.when(now < steps - SAME)
+            def _():
+                issue_same(now + SAME)
+
+            @pl.when(now >= LATE)
+            def _():
+                pass_on(now - LATE)
+
+            @pl.when(now < steps)
+            def _():
+                landed(now, 0)
+                update(now, False)
+
+            pick_now(now)
 
     @pl.when(away)
     def _():
-        @pl.loop(AHEAD, AHEAD + LEAD)
+        def both(step):
+            issue_inward(step)
+            apart_plain(step)
+
+        for step in range(AHEAD):
+            first(step, both)
+        for step in range(AHEAD, LEAD):
+            first(step, issue_inward)
+        rest(LEAD)
+
+        @pl.loop(late, steps)
         def _(step):
-            issue_inward(step)
+            combine(step, apart_cols)
+
+        forward().start()
+
+        @pl.loop(0, last)
+        def _(now):
+            @pl.when(now < late - AHEAD)
+            def _():
+                apart_plain(now + AHEAD)
+
+            @pl.when(now < steps - LEAD)
+            def _():
+                issue_inward(now + LEAD)
+
+            @pl.when(now < late)
+            def _():
+                landed(now, 0)
+                cross(now).wait_recv()
+                update(now, True)
+
+            @pl.when((now >= late) & (now < steps))
+            def _():
+                landed(now, 0)
+                update(now, False)
+
+            @pl.when(now >= LATE)
+            def _():
+                pass_on(now - LATE)
+
+            pick_now(now)
+
+    arrived(theirs, swap_send)
+
+    @pl.when(away)
+    def _():
+        arrived(mine.at[kept, apart_cols], apart_send)
+        arrived(inward, inward_send)
+        forward().wait_send()
 
     @pl.when(home)
     def _():
-        @pl.loop(0, AHEAD)
-        def _(step):
-            issue_same(step)
-
-    @pl.loop(0, steps + LATE)
-    def _(now):
-        @pl.when(home & (now < steps))
-        def _():
-            landed(now, 1)
-            cross(now).start()
-
-        @pl.when(home & (now < steps - AHEAD))
-        def _():
-            fetch(now + AHEAD)
-            issue_apart(now + AHEAD)
-            issue_same(now + AHEAD)
-
-        @pl.when(away & (now < steps - AHEAD))
-        def _():
-            issue_apart(now + AHEAD)
-
-        @pl.when(away & (now < steps - AHEAD - LEAD))
-        def _():
-            issue_inward(now + AHEAD + LEAD)
-
-        @pl.when(home & (now < steps))
-        def _():
-            landed(now, 0)
-            update(now, False)
-
-        @pl.when(away & (now < steps))
-        def _():
-            landed(now, 0)
-            cross(now).wait_recv()
-            update(now, True)
-
-        @pl.when(now >= LATE)
-        def _():
-            to_far(far, now - LATE).wait_recv()
-            relay(far, now - LATE).start()
-
-    @pl.loop(0, steps)
-    def _(step):
-        swap(step).wait_send()
-        sent = mine.at[rows(step), apart_cols]
-        arrived(sent, apart_send.at[step])
-
-        @pl.when(away)
-        def _():
-            inbound(step).wait_send()
-
-        @pl.when(home)
-        def _():
-            cross(step).wait_send()
-
-        @pl.when(home & (owner_core == core))
-        def _():
-            part = mine.at[rows(step), pl.ds(0, span - width)]
-            arrived(part, same_send.at[step])
-
-        @pl.when(home & (owner_core != core))
-        def _():
-            part = mine.at[rows(step), pl.ds(0, span)]
-            arrived(part, same_send.at[step])
-
-        to_far(rank, step).wait_send()
-        to_near(rank, step).wait_send()
-        to_near(near, step).wait_recv()
-        relay(far, step).wait_send()
-        relay((1 - row) * 2 + 1 - core, step).wait_recv()
+        arrived(mine.at[:, apart_cols], apart_send)
+        arrived(land.at[1, :, :, kept], cross_send)
+
+    @pl.when(home & (owner_core == core))
+    def _():
+        arrived(mine.at[:, pl.ds(0, span - width)], same_send)
+
+    @pl.when(home & (owner_core != core))
+    def _():
+        arrived(mine.at[:, pl.ds(0, span)], same_send)
+
+    own = roll.at[:, pl.ds(rank * subs, subs)]
+    arrived(own, far_send)
+    arrived(own, near_send)
+    arrived(own, relay_send)
+    arrived(roll.at[:, pl.ds(near * subs, subs)], near_recv)
+    arrived(roll.at[:, pl.ds(across * subs, subs)], relay_recv)
 
 
 def finish_kernel(
@@ -473,20 +545,32 @@
         scratch_shapes=[
             pltpu.VMEM((slab, hidden_width), half),
             pltpu.VMEM((slab, hidden_width), half),
+            pltpu.VMEM((READY * CHUNK, hidden_width), half),
             pltpu.VMEM((2, subs, 2, slab, width), half),
             pltpu.VMEM((slab, hidden_width // 2), half),
+            pltpu.VMEM((PRE * CHUNK, hidden_width // 2), half),
             pltpu.VMEM(tokens.shape, half),
             pltpu.VMEM((routed, tokens.shape[0]), half),
+            dma((3,)),
+            dma,
+            dma((len(SWAPS) + 1,)),
+            dma((3,)),
+            dma,
+            dma,
+            dma,
+            dma((2 * steps,)),
+            dma,
             dma((steps,)),
+            dma,
+            dma,
+            dma,
+            dma,
+            dma,
+            dma,
             dma((steps,)),
-            dma((steps,)),
-            dma((3 * steps,)),
-            dma,
-            dma((steps,)),
-            dma((steps,)),
-            dma((2 * steps,)),
-        ]
-        + [dma((steps,))] * 10,
+            dma,
+            dma,
+        ],
         compiler_params=pltpu.CompilerParams(
             has_side_effects=True, collective_id=0, vmem_limit_bytes=42 * 1024 * 1024
         ),
@@ -519,7 +603,8 @@
         and tensor_count % rank_count == 0
         and slab % LANES == 0
         and slab % CHUNK == 0
-        and slab // CHUNK > AHEAD + LEAD
+        and slab // CHUNK > max(LEAD, *SWAPS, AHEAD + PRE)
+        and tokens.shape[1] // (tensor_count * LANES) + PICK <= slab // CHUNK
         and tokens.shape[1] % (tensor_count * LANES) == 0
         and hidden_width % (tensor_count * LANES) == 0
     )

time: 113 us -> 103 us (0.912)
  Pallas kernels: 113 us -> 102 us
    pallas_call x1, Pallas kernels: 106 us -> 95.5 us  [fused(): pl.pallas_call(functools.partial(reduce_kernel, tensor_count), out_shape=...]
where the time goes in v2:
time: 103 us
  Pallas kernels  102 us (99%)
    pallas_call x1, Pallas kernels, fused(): pl.pallas_call(functools.partial(reduce_kernel, tensor_count), out_shape=...  95.5 us
    pallas_call x1, Pallas kernels, fused(): pl.pallas_call(finish_kernel, out_shape=[pltpu.HBM(whole, f32)] * 3 + [pl...  6.49 us

profile of v2, /device:TPU:0, one launch (start us, length us, event | category | flops | bytes accessed | tf_op | source)
XLA Modules:
  0.0 102.6 jit_solution(962884602833908255)
XLA Ops:
  0.6 95.5 %shard_map.101 = (f32[2,2,896,256]{3,2,1,0:T(8,128)S(1)}, f32[2,2,896,256]{3,2,1,0:T(8,128)S(1)}, f32[2,2,896,256]{3,2,1,0:T(8,128)S(1)}, bf16[2,8,896,256]{3,2,1,0:T(8,128)(2,1)S(1)}, bf16[128,7168]{1,0:T(8,128)(2,1)S(1)}) custom-call(bf16[1,2,896,2048]{3,2,1,0:T(8,128)(2,1)} %grads.1, f32[2,2,896,256]{3,2,1,0:T(8,128)} %bitcast.12, ...), custom_call_target="tpu_custom_call" | custom-call | tf_op jit(solution)/shard_map/pallas_call | solution.py:536
  96.1 6.5 %shard_map.102 = (f32[2,1792,256]{2,1,0:T(8,128)}, f32[2,1792,256]{2,1,0:T(8,128)}, f32[2,1792,256]{2,1,0:T(8,128)}, bf16[2,7168,256]{2,1,0:T(8,128)(2,1)}, bf16[128,256]{1,0:T(8,128)(2,1)}) custom-call(f32[2,1792,256]{2,1,0:T(8,128)S(1)} %bitcast.9, f32[2,1792,256]{2,1,0:T(8,128)S(1)} %bitcast.10, f32[2,1792,256]{2,1,0:T(8,128)S(1)} %bitcast.11, ...), custom_call_target="tpu_custom_call" | custom-call | tf_op jit(solution)/shard_map/pallas_call | solution.py:582

commit v3 on v2

--- a/solution.py
+++ b/solution.py
@@ -76,11 +76,13 @@
     early,
     token_rows,
     chosen,
+    table,
     load_sem,
     swap_send,
     swap_recv,
     state_sem,
     token_sem,
+    table_sem,
     apart_send,
     same_send,
     land_recv,
@@ -313,14 +315,9 @@
 
     load(0).start()
     bring().start()
-    load(1).start()
-    for which in range(3):
-        state(which).start()
     token_copy = pltpu.make_async_copy(tokens, token_rows, token_sem)
-    token_copy.start()
-    index = lax.broadcasted_iota(jnp.int32, (token_rows.shape[0], route.shape[1]), 0)
-    onehot = jnp.where(index == route[...], 1.0, 0.0)
-    chosen[...] = onehot.T.astype(chosen.dtype)
+    table_copy = pltpu.make_async_copy(route, table, table_sem)
+    table_copy.start()
     wide = tensor_count * LANES
     picks = token_rows.shape[1] // wide
 
@@ -333,6 +330,10 @@
         @pl.when(now == PICK)
         def _():
             token_copy.wait()
+            table_copy.wait()
+            index = lax.broadcasted_iota(jnp.int32, (token_rows.shape[0], table.shape[1]), 0)
+            onehot = jnp.where(index == table[...], 1.0, 0.0)
+            chosen[...] = onehot.T.astype(chosen.dtype)
 
         @pl.when((now >= PICK) & (now < PICK + picks))
         def _():
@@ -343,6 +344,10 @@
     pl.semaphore_wait(barrier, peers)
     for piece in range(len(pieces)):
         swap(piece).start()
+    load(1).start()
+    for which in range(3):
+        state(which).start()
+    token_copy.start()
 
     def first(step, action):
         for piece, (start, _) in enumerate(pieces):
@@ -369,11 +374,9 @@
     def _():
         for step in range(AHEAD):
             first(step, apart_plain)
+        for step in range(SAME):
+            issue_same(step)
         rest(AHEAD)
-
-        @pl.loop(0, SAME)
-        def _(step):
-            issue_same(step)
 
         @pl.loop(0, last)
         def _(now):
@@ -540,7 +543,7 @@
             pltpu.VMEM((2, tensor_count, slab, width), half),
             pltpu.VMEM((routed, depth), half),
         ],
-        in_specs=[anywhere] * 5 + [vmem],
+        in_specs=[anywhere] * 6,
         out_specs=[vmem] * 5,
         scratch_shapes=[
             pltpu.VMEM((slab, hidden_width), half),
@@ -551,10 +554,12 @@
             pltpu.VMEM((PRE * CHUNK, hidden_width // 2), half),
             pltpu.VMEM(tokens.shape, half),
             pltpu.VMEM((routed, tokens.shape[0]), half),
+            pltpu.VMEM((1, routed), jnp.int32),
             dma((3,)),
             dma,
             dma((len(SWAPS) + 1,)),
             dma((3,)),
+            dma,
             dma,
             dma,
             dma,

time: 103 us -> 102 us (level)
  no operation moved by 1% of the time
where the time goes in v3:
time: 102 us
  Pallas kernels  101 us (99%)
    pallas_call x1, Pallas kernels, fused(): pl.pallas_call(functools.partial(reduce_kernel, tensor_count), out_shape=...  94.9 us
    pallas_call x1, Pallas kernels, fused(): pl.pallas_call(finish_kernel, out_shape=[pltpu.HBM(whole, f32)] * 3 + [pl...  6.49 us

profile of v3, /device:TPU:0, one launch (start us, length us, event | category | flops | bytes accessed | tf_op | source)
XLA Modules:
  0.0 102.0 jit_solution(8842132300300761445)
XLA Ops:
  0.6 94.9 %shard_map.101 = (f32[2,2,896,256]{3,2,1,0:T(8,128)S(1)}, f32[2,2,896,256]{3,2,1,0:T(8,128)S(1)}, f32[2,2,896,256]{3,2,1,0:T(8,128)S(1)}, bf16[2,8,896,256]{3,2,1,0:T(8,128)(2,1)S(1)}, bf16[128,7168]{1,0:T(8,128)(2,1)S(1)}) custom-call(bf16[1,2,896,2048]{3,2,1,0:T(8,128)(2,1)} %grads.1, f32[2,2,896,256]{3,2,1,0:T(8,128)} %bitcast.12, ...), custom_call_target="tpu_custom_call" | custom-call | tf_op jit(solution)/shard_map/pallas_call | solution.py:539
  95.5 6.5 %shard_map.102 = (f32[2,1792,256]{2,1,0:T(8,128)}, f32[2,1792,256]{2,1,0:T(8,128)}, f32[2,1792,256]{2,1,0:T(8,128)}, bf16[2,7168,256]{2,1,0:T(8,128)(2,1)}, bf16[128,256]{1,0:T(8,128)(2,1)}) custom-call(f32[2,1792,256]{2,1,0:T(8,128)S(1)} %bitcast.9, f32[2,1792,256]{2,1,0:T(8,128)S(1)} %bitcast.10, f32[2,1792,256]{2,1,0:T(8,128)S(1)} %bitcast.11, ...), custom_call_target="tpu_custom_call" | custom-call | tf_op jit(solution)/shard_map/pallas_call | solution.py:587

commit v4 on v3

--- a/solution.py
+++ b/solution.py
@@ -182,7 +182,7 @@
             mine.at[rows(step), columns(goal)],
             land.at[slot, sub, core, rows(step)],
             apart_send,
-            land_recv.at[slot * steps + step],
+            land_recv.at[step],
             row * 2 + owner_core,
             goal,
         )
@@ -205,13 +205,16 @@
             land_recv.at[step],
         )
 
-    def landed(step, part):
-        arrived(land.at[part, :, :, rows(step)], land_recv.at[part * steps + step])
+    def landed(step):
+        arrived(land.at[:, :, :, rows(step)], land_recv.at[step])
+
+    def landed_own(step):
+        arrived(land.at[0, :, :, rows(step)], land_recv.at[step])
 
     def cross(step):
         return remote(
             land.at[1, :, :, rows(step)], land.at[1, :, :, rows(step)],
-            cross_send, land_recv.at[steps + step], far, place,
+            cross_send, land_recv.at[step], far, place,
         )
 
     def block(of_rank, step):
@@ -382,7 +385,7 @@
         def _(now):
             @pl.when(now < late)
             def _():
-                landed(now, 1)
+                landed(now)
                 cross(now).start()
 
             @pl.when(now < late - AHEAD)
@@ -406,9 +409,12 @@
             def _():
                 pass_on(now - LATE)
 
+            @pl.when((now >= late) & (now < steps))
+            def _():
+                landed_own(now)
+
             @pl.when(now < steps)
             def _():
-                landed(now, 0)
                 update(now, False)
 
             pick_now(now)
@@ -443,13 +449,12 @@
 
             @pl.when(now < late)
             def _():
-                landed(now, 0)
-                cross(now).wait_recv()
+                landed(now)
                 update(now, True)
 
             @pl.when((now >= late) & (now < steps))
             def _():
-                landed(now, 0)
+                landed_own(now)
                 update(now, False)
 
             @pl.when(now >= LATE)
@@ -493,9 +498,14 @@
     copies = []
     for source, target in ((held0, out0), (held1, out1), (held2, out2), (roll, full)):
         for half in range(2):
-            copies.append(
-                pltpu.make_async_copy(source.at[half], target.at[half], sems.at[len(copies)])
-            )
+            size = source.shape[1] // 4
+            for part in range(4):
+                at = pl.ds(part * size, size)
+                copies.append(
+                    pltpu.make_async_copy(
+                        source.at[half, at], target.at[half, at], sems.at[len(copies)]
+                    )
+                )
     for copy in copies:
         copy.start()
     acc[...] = jnp.zeros_like(acc)
@@ -563,7 +573,7 @@
             dma,
             dma,
             dma,
-            dma((2 * steps,)),
+            dma((steps,)),
             dma,
             dma((steps,)),
             dma,
@@ -593,7 +603,7 @@
         scratch_shapes=[
             pltpu.VMEM((2, routed, width), f32),
             pltpu.VMEM((routed, width), half),
-            dma((9,)),
+            dma((33,)),
         ],
         compiler_params=pltpu.CompilerParams(vmem_limit_bytes=8 * 1024 * 1024),
     )(*held, roll.reshape(wide), picked)

time: 102 us -> 102 us (level)
  no operation moved by 1% of the time
where the time goes in v4:
time: 102 us
  Pallas kernels  101 us (99%)
    pallas_call x1, Pallas kernels, fused(): pl.pallas_call(functools.partial(reduce_kernel, tensor_count), out_shape=...  94.6 us
    pallas_call x1, Pallas kernels, fused(): pl.pallas_call(finish_kernel, out_shape=[pltpu.HBM(whole, f32)] * 3 + [pl...  6.59 us

profile of v4, /device:TPU:0, one launch (start us, length us, event | category | flops | bytes accessed | tf_op | source)
XLA Modules:
  0.0 101.9 jit_solution(8435768070976618530)
XLA Ops:
  0.6 94.6 %shard_map.101 = (f32[2,2,896,256]{3,2,1,0:T(8,128)S(1)}, f32[2,2,896,256]{3,2,1,0:T(8,128)S(1)}, f32[2,2,896,256]{3,2,1,0:T(8,128)S(1)}, bf16[2,8,896,256]{3,2,1,0:T(8,128)(2,1)S(1)}, bf16[128,7168]{1,0:T(8,128)(2,1)S(1)}) custom-call(bf16[1,2,896,2048]{3,2,1,0:T(8,128)(2,1)} %grads.1, f32[2,2,896,256]{3,2,1,0:T(8,128)} %bitcast.12, ...), custom_call_target="tpu_custom_call" | custom-call | tf_op jit(solution)/shard_map/pallas_call | solution.py:549
  95.3 6.6 %shard_map.102 = (f32[2,1792,256]{2,1,0:T(8,128)}, f32[2,1792,256]{2,1,0:T(8,128)}, f32[2,1792,256]{2,1,0:T(8,128)}, bf16[2,7168,256]{2,1,0:T(8,128)(2,1)}, bf16[128,256]{1,0:T(8,128)(2,1)}) custom-call(f32[2,1792,256]{2,1,0:T(8,128)S(1)} %bitcast.9, f32[2,1792,256]{2,1,0:T(8,128)S(1)} %bitcast.10, f32[2,1792,256]{2,1,0:T(8,128)S(1)} %bitcast.11, ...), custom_call_target="tpu_custom_call" | custom-call | tf_op jit(solution)/shard_map/pallas_call | solution.py:597
